TPU v7x, 32 devices: a whole 2x2x4 slice. The times are simulated.
32 devices in a mesh: tm: 8 (over z, y), space: 4 (over x, core).
Axes of the slice: x: 2, y: 2, z: 4, core: 2. Of those that a mesh axis runs over, the one named last changes fastest.
Arguments:
- observed: float32 [64, 512, 128], P('tm', 'space'), may hold values from -6 to 6
- gain: float32 [4, 128, 128], P('space'), may hold values from -0.15625 to 0.15625
- trans: float32 [4, 384, 128], P('space'), may hold values from -1 to 1
- dynamics: float32 [4, 384, 128], P('space'), may hold values from -1 to 1
- smooth_gain: float32 [4, 384, 128], P('space'), may hold values from -1 to 1
Outputs:
- filtered: float32 [64, 512, 128], P('tm', 'space')
- smoothed: float32 [64, 512, 128], P('tm', 'space')
All inputs are finite; a program needn't handle non-finite values.
Results may differ from a plain program's by a relative error of at most 0.00017.
Values sent between devices are 32-bit elements; how exact they have to be, the bound alone decides.
A program may use at most 128 MiB of HBM per device.

v0:
```python
from functools import partial

import jax
import jax.numpy as jnp
from jax import lax
from jax.sharding import PartitionSpec as P

highest_mode = lax.Precision.HIGHEST


def shifted(shard, axis, by):
    devices = lax.axis_size(axis)
    pairs = [(i, i + by) for i in range(devices) if 0 <= i + by < devices]
    return lax.ppermute(shard, axis, pairs)


def apply_full(banded, current):
    count_tiles = banded.shape[0]
    tile_width = banded.shape[2]
    blocks = current.reshape(current.shape[0], count_tiles, tile_width, current.shape[2])
    empty_tile = jnp.zeros_like(blocks[:, :1])
    padded = jnp.concatenate([empty_tile, blocks, empty_tile], 1)
    stacked = jnp.concatenate([padded[:, :-2], padded[:, 1:-1], padded[:, 2:]], 2)
    result = jnp.einsum("crs,ncre->ncse", banded, stacked, precision=highest_mode)
    return result.reshape(current.shape)


def sweep(apply_step, inputs, entry, backward):
    length = inputs.shape[0]
    order = list(range(length - 1, -1, -1)) if backward else list(range(length))
    current = entry
    outputs = [entry] * length
    for moment in order:
        current = apply_step(current[None])[0] + inputs[moment]
        outputs[moment] = current
    return jnp.stack(outputs)


def carry_prefix(carry, tables, which, direction):
    total = carry
    for level in range(len(tables) + 1):
        reach = direction * (1 if level == 0 else 2 ** (level - 1))
        moved = shifted(total, "tm", reach)
        if level == 0:
            total = moved
        else:
            table = tables[level - 1][which]

            def term(start, count, table=table, moved=moved):
                return lax.dot_general(
                    table, moved, (((0,), (0,)), ((), ())), precision=highest_mode
                )

            total = total + lax.psum_scatter(
                term(jnp.int32(0), moved.shape[0] * lax.axis_size("space")),
                "space",
                scatter_dimension=0,
                tiled=True,
            )
    return total


def body(observed, gain, trans, dynamics, smooth_gain):
    steps, tile_width, members = observed.shape
    count_tiles = lax.axis_size("space")
    ranks = lax.axis_size("tm")
    place = lax.axis_index("tm")
    column = lax.axis_index("space")
    state_width = tile_width * count_tiles
    block_cols = state_width // ranks
    sections = (ranks - 1).bit_length()
    log_steps = steps.bit_length() - 1
    forcing = jnp.einsum("os,toe->tse", gain[0], observed, precision=highest_mode)
    full_trans, full_smooth, full_dynamics = (
        lax.all_gather(trans, "space", axis=0, tiled=True),
        lax.all_gather(smooth_gain, "space", axis=0, tiled=True),
        lax.all_gather(dynamics, "space", axis=0, tiled=True),
    )

    def first_block(full):
        target = place * block_cols // tile_width
        offset = place * block_cols % tile_width
        index = jnp.clip(target, 0, full.shape[0] - 1)
        slab = lax.dynamic_index_in_dim(full, index, 0, keepdims=False)
        row_start = jnp.clip(column - target + 1, 0, 2) * tile_width
        piece = lax.dynamic_slice(slab, (row_start, offset), (tile_width, block_cols))
        inside = (jnp.abs(column - target) <= 1).astype(jnp.float32)
        return piece * inside

    blocks = (first_block(full_trans), first_block(full_smooth))
    needed = []
    for level in range(log_steps + sections - 1):
        col_trans = lax.all_gather(blocks[0], "space", axis=0, tiled=True)
        col_smooth = lax.all_gather(blocks[1], "space", axis=0, tiled=True)
        blocks = (
            jnp.dot(
                lax.all_gather(blocks[0], "tm", axis=1, tiled=True),
                col_trans,
                precision=highest_mode,
            ),
            jnp.dot(
                lax.all_gather(blocks[1], "tm", axis=1, tiled=True),
                col_smooth,
                precision=highest_mode,
            ),
        )
        if level + 1 >= log_steps:
            needed.append(blocks)
    tables = []
    for pair in needed:
        tables.append(
            (
                lax.all_gather(pair[0], "tm", axis=1, tiled=True),
                lax.all_gather(pair[1], "tm", axis=1, tiled=True),
            )
        )
    final_moment = jnp.arange(steps)[:, None, None] == steps - 1
    at_end = jnp.logical_and(final_moment, place == ranks - 1)
    whole_forcing = lax.all_gather(forcing, "space", axis=1, tiled=True)
    zero_full = jnp.zeros((state_width, members), jnp.float32)
    step_trans = partial(apply_full, full_trans)
    step_smooth = partial(apply_full, full_smooth)
    trial = sweep(step_trans, whole_forcing, zero_full, False)
    own_tail = lax.dynamic_slice_in_dim(trial[steps - 1], column * tile_width, tile_width, 0)
    entry = carry_prefix(own_tail, tables, 0, 1)
    entry_full = lax.all_gather(entry, "space", axis=0, tiled=True)
    filtered_full = sweep(step_trans, whole_forcing, entry_full, False)
    mixed_full = apply_full(full_smooth, apply_full(full_dynamics, filtered_full))
    innovation_full = jnp.where(at_end, filtered_full, filtered_full - mixed_full)
    trial_back = sweep(step_smooth, innovation_full, zero_full, True)
    own_head = lax.dynamic_slice_in_dim(trial_back[0], column * tile_width, tile_width, 0)
    exit_state = carry_prefix(own_head, tables, 1, -1)
    exit_full = lax.all_gather(exit_state, "space", axis=0, tiled=True)
    smoothed_full = sweep(step_smooth, innovation_full, exit_full, True)
    filtered = lax.dynamic_slice_in_dim(filtered_full, column * tile_width, tile_width, 1)
    smoothed = lax.dynamic_slice_in_dim(smoothed_full, column * tile_width, tile_width, 1)
    return (filtered, smoothed)


def solution(mesh):
    return jax.shard_map(
        body,
        mesh=mesh,
        in_specs=(
            P("tm", "space", None),
            P("space", None, None),
            P("space", None, None),
            P("space", None, None),
            P("space", None, None),
        ),
        out_specs=(P("tm", "space", None), P("tm", "space", None)),
        check_vma=False,
    )
```

profile of v0, /device:TPU:15, one launch (start us, length us, event | category | flops | bytes accessed | tf_op | source)
XLA Modules:
  0.0 761.2 jit_solution(14386908536317861910)
XLA Ops:
  27.8 22.3 %all-gather = f32[1,128,512]{1,0,2:T(1,128)S(1)} all-gather(f32[1,128,64]{1,0,2:T(1,128)S(1)} %copy.199), channel_id=2, replica_groups=mesh['tm'=8,'space'=4] {'tm'}, dimensions={2}, use_global_device_ids=true | all-gather | bytes 294912 | tf_op jit(solution)/shard_map/all_gather | solution.py:97
  50.6 11.4 %all_gather.93 = f32[512,64]{0,1:T(8,128)S(1)} all-gather(f32[128,64]{0,1:T(8,128)S(1)} %fusion.174), channel_id=1, replica_groups=mesh['tm'=8,'space'=4] {'space'}, dimensions={0}, use_global_device_ids=true | all-gather | bytes 163840 | tf_op jit(solution)/shard_map/all_gather | solution.py:93
  62.0 24.7 %all_gather.92 = f32[128,512]{0,1:T(8,128)S(1)} all-gather(f32[128,64]{0,1:T(8,128)S(1)} %fusion.174), channel_id=1, replica_groups=mesh['tm'=8,'space'=4] {'tm'}, dimensions={1}, use_global_device_ids=true | all-gather | bytes 294912 | tf_op jit(solution)/shard_map/all_gather | solution.py:97
  87.1 11.4 %all_gather.95 = f32[512,64]{0,1:T(8,128)S(1)} all-gather(f32[128,64]{0,1:T(8,128)S(1)} %fusion.211), channel_id=1, replica_groups=mesh['tm'=8,'space'=4] {'space'}, dimensions={0}, use_global_device_ids=true | all-gather | bytes 163840 | tf_op jit(solution)/shard_map/all_gather | solution.py:93
  98.5 24.7 %all_gather.94 = f32[128,512]{0,1:T(8,128)S(1)} all-gather(f32[128,64]{0,1:T(8,128)S(1)} %fusion.211), channel_id=1, replica_groups=mesh['tm'=8,'space'=4] {'tm'}, dimensions={1}, use_global_device_ids=true | all-gather | bytes 294912 | tf_op jit(solution)/shard_map/all_gather | solution.py:97
  123.6 14.5 %all_gather.102 = f32[4,384,128]{2,1,0:T(8,128)S(1)} all-gather(f32[1,384,128]{2,1,0:T(8,128)S(1)} %copy-done.47), channel_id=1, replica_groups=mesh['tm'=8,'space'=4] {'space'}, dimensions={0}, use_global_device_ids=true | all-gather | bytes 983040 | tf_op jit(solution)/shard_map/all_gather | solution.py:76
  169.5 23.7 %all_gather.96 = f32[128,512]{0,1:T(8,128)S(1)} all-gather(f32[128,64]{0,1:T(8,128)S(1)} %fusion.212), channel_id=1, replica_groups=mesh['tm'=8,'space'=4] {'tm'}, dimensions={1}, use_global_device_ids=true | all-gather | bytes 294912 | tf_op jit(solution)/shard_map/all_gather | solution.py:113
  193.3 12.1 %all_gather.97 = f32[512,64]{0,1:T(8,128)S(1)} all-gather(f32[128,64]{0,1:T(8,128)S(1)} %fusion.212), channel_id=1, replica_groups=mesh['tm'=8,'space'=4] {'space'}, dimensions={0}, use_global_device_ids=true | all-gather | bytes 163840 | tf_op jit(solution)/shard_map/all_gather | solution.py:93
  219.3 24.0 %all_gather.98 = f32[128,512]{0,1:T(8,128)S(1)} all-gather(f32[128,64]{0,1:T(8,128)S(1)} %fusion.214), channel_id=1, replica_groups=mesh['tm'=8,'space'=4] {'tm'}, dimensions={1}, use_global_device_ids=true | all-gather | bytes 294912 | tf_op jit(solution)/shard_map/all_gather | solution.py:113
  243.3 24.7 %all-gather.2 = f32[1,128,512]{1,0,2:T(1,128)S(1)} all-gather(f32[1,128,64]{1,0,2:T(1,128)S(1)} %copy.255), channel_id=4, replica_groups=mesh['tm'=8,'space'=4] {'tm'}, dimensions={2}, use_global_device_ids=true | all-gather | bytes 294912 | tf_op jit(solution)/shard_map/all_gather | solution.py:102
  273.3 24.0 %all_gather.106 = f32[128,512]{0,1:T(8,128)} all-gather(f32[128,64]{0,1:T(8,128)S(1)} %fusion.172), channel_id=1, replica_groups=mesh['tm'=8,'space'=4] {'tm'}, dimensions={1}, use_global_device_ids=true | all-gather | bytes 294912 | tf_op jit(solution)/shard_map/all_gather | solution.py:102
  298.5 24.0 %all_gather.99 = f32[512,64]{0,1:T(8,128)S(1)} all-gather(f32[128,64]{0,1:T(8,128)S(1)} %fusion.214), channel_id=1, replica_groups=mesh['tm'=8,'space'=4] {'space'}, dimensions={0}, use_global_device_ids=true | all-gather | bytes 163840 | tf_op jit(solution)/shard_map/all_gather | solution.py:93
  344.7 19.6 %all_gather.100 = f32[128,512]{0,1:T(8,128)S(1)} all-gather(f32[128,64]{0,1:T(8,128)S(1)} %fusion.216), channel_id=1, replica_groups=mesh['tm'=8,'space'=4] {'tm'}, dimensions={1}, use_global_device_ids=true | all-gather | bytes 294912 | tf_op jit(solution)/shard_map/all_gather | solution.py:113
  365.5 12.4 %all_gather.109 = f32[512,64]{0,1:T(8,128)S(1)} all-gather(f32[128,64]{0,1:T(8,128)} %fusion.218), channel_id=1, replica_groups=mesh['tm'=8,'space'=4] {'space'}, dimensions={0}, use_global_device_ids=true | all-gather | bytes 163840 | tf_op jit(solution)/shard_map/all_gather | solution.py:94
  377.9 26.9 %all_gather.108 = f32[128,512]{0,1:T(8,128)} all-gather(f32[128,64]{0,1:T(8,128)} %fusion.218), channel_id=1, replica_groups=mesh['tm'=8,'space'=4] {'tm'}, dimensions={1}, use_global_device_ids=true | all-gather | bytes 294912 | tf_op jit(solution)/shard_map/all_gather | solution.py:102
  404.8 15.7 %all_gather.103 = f32[4,384,128]{2,1,0:T(8,128)} all-gather(f32[1,384,128]{2,1,0:T(8,128)} %param.8), channel_id=1, replica_groups=mesh['tm'=8,'space'=4] {'space'}, dimensions={0}, use_global_device_ids=true | all-gather | bytes 983040 | tf_op jit(solution)/shard_map/all_gather | solution.py:77
  544.8 22.0 %all_gather.110 = f32[128,512]{0,1:T(8,128)S(1)} all-gather(f32[128,64]{0,1:T(8,128)S(1)} %fusion.219), channel_id=1, replica_groups=mesh['tm'=8,'space'=4] {'tm'}, dimensions={1}, use_global_device_ids=true | all-gather | bytes 294912 | tf_op jit(solution)/shard_map/all_gather | solution.py:114
  568.0 12.7 %all_gather.111 = f32[512,64]{0,1:T(8,128)S(1)} all-gather(f32[128,64]{0,1:T(8,128)S(1)} %fusion.219), channel_id=1, replica_groups=mesh['tm'=8,'space'=4] {'space'}, dimensions={0}, use_global_device_ids=true | all-gather | bytes 163840 | tf_op jit(solution)/shard_map/all_gather | solution.py:94
  581.0 16.3 %reduce-scatter.13.cloned.1.call-done = f32[128,128]{0,1:T(8,128)} async-done(((f32[512,128]{0,1:T(8,128)}), f32[128,128]{0,1:T(8,128)}) %reduce-scatter.13.cloned.1.call-update) | async-done | bytes 65552 | tf_op jit(solution)/shard_map/reduce_scatter | solution.py:54
  600.4 22.2 %all_gather.112 = f32[128,512]{0,1:T(8,128)S(1)} all-gather(f32[128,64]{0,1:T(8,128)S(1)} %fusion.221), channel_id=1, replica_groups=mesh['tm'=8,'space'=4] {'tm'}, dimensions={1}, use_global_device_ids=true | all-gather | bytes 294912 | tf_op jit(solution)/shard_map/all_gather | solution.py:114
  623.7 12.3 %all_gather.113 = f32[512,64]{0,1:T(8,128)S(1)} all-gather(f32[128,64]{0,1:T(8,128)S(1)} %fusion.221), channel_id=1, replica_groups=mesh['tm'=8,'space'=4] {'space'}, dimensions={0}, use_global_device_ids=true | all-gather | bytes 163840 | tf_op jit(solution)/shard_map/all_gather | solution.py:94
  636.3 16.4 %reduce-scatter.15.cloned.1.call-done = f32[128,128]{0,1:T(8,128)} async-done(((f32[512,128]{0,1:T(8,128)}), f32[128,128]{0,1:T(8,128)}) %reduce-scatter.15.cloned.1.call-update) | async-done | bytes 65552 | tf_op jit(solution)/shard_map/reduce_scatter | solution.py:54
  654.9 22.9 %all_gather.114 = f32[128,512]{0,1:T(8,128)S(1)} all-gather(f32[128,64]{0,1:T(8,128)S(1)} %fusion.223), channel_id=1, replica_groups=mesh['tm'=8,'space'=4] {'tm'}, dimensions={1}, use_global_device_ids=true | all-gather | bytes 294912 | tf_op jit(solution)/shard_map/all_gather | solution.py:114
  682.8 25.3 %reduce-scatter.17.cloned.1.call-done = f32[128,128]{0,1:T(8,128)} async-done(((f32[512,128]{0,1:T(8,128)}), f32[128,128]{0,1:T(8,128)}) %reduce-scatter.17.cloned.1.call-update) | async-done | bytes 65552 | tf_op jit(solution)/shard_map/reduce_scatter | solution.py:54
  (315 shorter events, 279.3 us)
Async XLA Ops:
  7.2 130.9 %all-gather.6.cloned.1.call-start = ((), (), s32[]{:S(2)}) async-start(), calls=%async_computation.6 | async-start | bytes 2621440 | tf_op jit(solution)/shard_map/all_gather | solution.py:119
  10.9 257.8 %reduce-scatter.7.cloned.1.call-start = ((), (), s32[]{:S(2)}) async-start(), calls=%async_computation.7 | async-start | bytes 327680 | tf_op jit(solution)/shard_map/reduce_scatter | solution.py:54
  19.9 103.7 %copy-start.47 = (f32[1,384,128]{2,1,0:T(8,128)S(1)}, f32[1,384,128]{2,1,0:T(8,128)}, u32[]{:S(2)}) copy-start(f32[1,384,128]{2,1,0:T(8,128)} %param.9) | copy-start | bytes 589828
  123.2 17.6 %copy-start.3 = (f32[1,4,128,128]{3,2,1,0:T(8,128)}, f32[1,4,128,128]{3,2,1,0:T(8,128)S(1)}, u32[]{:S(2)}) copy-start(f32[1,4,128,128]{3,2,1,0:T(8,128)S(1)} %pad_slice_fusion.64) | copy-start | bytes 786436
  167.6 37.7 %collective-permute-start = (f32[128,128]{0,1:T(8,128)S(1)}, f32[128,128]{0,1:T(8,128)S(1)}, u32[]{:S(2)}, u32[]{:S(2)}) collective-permute-start(f32[128,128]{0,1:T(8,128)S(1)} %dynamic-slice_add_fusion.1), channel_id=1, source_target_pairs={{0,4},{4,8},{8,12},{12,16},{16,20},{20,24},{24,28},{1,5},{5,9},{9,... | collective-permute-start | bytes 196616 | tf_op jit(solution)/shard_map/ppermute | solution.py:14
  205.3 7.6 %copy-start.48 = (f32[128,128]{0,1:T(8,128)}, f32[128,128]{0,1:T(8,128)S(1)}, u32[]{:S(2)}) copy-start(f32[128,128]{0,1:T(8,128)S(1)} %collective-permute-done) | copy-start | bytes 196612
  205.3 6.3 collective-permute-start.1
  212.7 126.4 %reduce-scatter.9.cloned.1.call-start = ((), (), s32[]{:S(2)}) async-start(), calls=%async_computation.8 | async-start | bytes 327680 | tf_op jit(solution)/shard_map/reduce_scatter | solution.py:54
  269.6 27.7 %collective-permute-start.2 = (f32[128,128]{0,1:T(8,128)S(1)}, f32[128,128]{0,1:T(8,128)S(1)}, u32[]{:S(2)}, u32[]{:S(2)}) collective-permute-start(f32[128,128]{0,1:T(8,128)S(1)} %add.374), channel_id=1, source_target_pairs={{0,8},{4,12},{8,16},{12,20},{16,24},{20,28},{1,9},{5,13},{9,17},{1... | collective-permute-start | bytes 196616 | tf_op jit(solution)/shard_map/ppermute | solution.py:14
  298.4 122.1 %reduce-scatter.11.cloned.1.call-start = ((), (), s32[]{:S(2)}) async-start(), calls=%async_computation.9 | async-start | bytes 327680 | tf_op jit(solution)/shard_map/reduce_scatter | solution.py:54
  340.6 23.7 %collective-permute-start.3 = (f32[128,128]{0,1:T(8,128)S(1)}, f32[128,128]{0,1:T(8,128)S(1)}, u32[]{:S(2)}, u32[]{:S(2)}) collective-permute-start(f32[128,128]{0,1:T(8,128)S(1)} %add.375), channel_id=1, source_target_pairs={{0,16},{4,20},{8,24},{12,28},{1,17},{5,21},{9,25},{13,29},{2,18},{... | collective-permute-start | bytes 196616 | tf_op jit(solution)/shard_map/ppermute | solution.py:14
  365.4 231.9 %reduce-scatter.13.cloned.1.call-start = ((), (), s32[]{:S(2)}) async-start(), calls=%async_computation.10 | async-start | bytes 327680 | tf_op jit(solution)/shard_map/reduce_scatter | solution.py:54
  534.6 6.3 collective-permute-start.4
  540.8 40.1 %copy-start.49 = (f32[128,128]{0,1:T(8,128)}, f32[128,128]{0,1:T(8,128)S(1)}, u32[]{:S(2)}) copy-start(f32[128,128]{0,1:T(8,128)S(1)} %collective-permute-done.4) | copy-start | bytes 196612
  540.8 26.0 %collective-permute-start.5 = (f32[128,128]{0,1:T(8,128)S(1)}, f32[128,128]{0,1:T(8,128)S(1)}, u32[]{:S(2)}, u32[]{:S(2)}) collective-permute-start(f32[128,128]{0,1:T(8,128)S(1)} %collective-permute-done.4), channel_id=1, source_target_pairs={{4,0},{8,4},{12,8},{16,12},{20,16},{24,20},{28,24},{5,1},{9,5},{13... | collective-permute-start | bytes 196616 | tf_op jit(solution)/shard_map/ppermute | solution.py:14
  567.9 84.8 %reduce-scatter.15.cloned.1.call-start = ((), (), s32[]{:S(2)}) async-start(), calls=%async_computation.11 | async-start | bytes 327680 | tf_op jit(solution)/shard_map/reduce_scatter | solution.py:54
  598.2 24.4 %collective-permute-start.6 = (f32[128,128]{0,1:T(8,128)S(1)}, f32[128,128]{0,1:T(8,128)S(1)}, u32[]{:S(2)}, u32[]{:S(2)}) collective-permute-start(f32[128,128]{0,1:T(8,128)S(1)} %add.400), channel_id=1, source_target_pairs={{8,0},{12,4},{16,8},{20,12},{24,16},{28,20},{9,1},{13,5},{17,9},{2... | collective-permute-start | bytes 196616 | tf_op jit(solution)/shard_map/ppermute | solution.py:14
  623.7 84.5 %reduce-scatter.17.cloned.1.call-start = ((), (), s32[]{:S(2)}) async-start(), calls=%async_computation.12 | async-start | bytes 327680 | tf_op jit(solution)/shard_map/reduce_scatter | solution.py:54
  653.6 24.2 %collective-permute-start.7 = (f32[128,128]{0,1:T(8,128)S(1)}, f32[128,128]{0,1:T(8,128)S(1)}, u32[]{:S(2)}, u32[]{:S(2)}) collective-permute-start(f32[128,128]{0,1:T(8,128)S(1)} %add.401), channel_id=1, source_target_pairs={{16,0},{20,4},{24,8},{28,12},{17,1},{21,5},{25,9},{29,13},{18,2},{... | collective-permute-start | bytes 196616 | tf_op jit(solution)/shard_map/ppermute | solution.py:14
  678.9 38.9 %copy-start.5 = (f32[1,512,128]{2,1,0:T(8,128)S(1)}, f32[1,512,128]{2,1,0:T(8,128)}, u32[]{:S(2)}) copy-start(f32[1,512,128]{2,1,0:T(8,128)} %copy.364) | copy-start | bytes 786436
  736.1 8.0 %copy-start.30 = (f32[4,128,128]{1,2,0:T(8,128)S(1)}, f32[4,128,128]{1,2,0:T(8,128)}, u32[]{:S(2)}) copy-start(f32[4,128,128]{1,2,0:T(8,128)} %get-tuple-element.125) | copy-start | bytes 786436
  736.1 8.9 %copy-start.29 = (f32[4,128,128]{1,2,0:T(8,128)S(1)}, f32[4,128,128]{1,2,0:T(8,128)}, u32[]{:S(2)}) copy-start(f32[4,128,128]{1,2,0:T(8,128)} %get-tuple-element.123) | copy-start | bytes 786436
  736.1 9.7 %copy-start.28 = (f32[4,128,128]{1,2,0:T(8,128)S(1)}, f32[4,128,128]{1,2,0:T(8,128)}, u32[]{:S(2)}) copy-start(f32[4,128,128]{1,2,0:T(8,128)} %get-tuple-element.121) | copy-start | bytes 786436
  738.0 8.7 %copy-start.27 = (f32[4,128,128]{1,2,0:T(8,128)S(1)}, f32[4,128,128]{1,2,0:T(8,128)}, u32[]{:S(2)}) copy-start(f32[4,128,128]{1,2,0:T(8,128)} %get-tuple-element.119) | copy-start | bytes 786436
  (41 other events, 123.3 us)
Sparse Core Ops, SparseCore 0:
  11.0 24.7 all-gather.5
  212.8 21.7 reduce-scatter.6
  298.5 40.5 reduce-scatter.8
  365.6 28.7 reduce-scatter.10
  568.0 29.2 reduce-scatter.12
  623.8 28.8 reduce-scatter.14
  679.0 29.0 reduce-scatter.16
where the time goes:
time: 769 us; the launch traced here: 761 us
  blocking collectives  450 us (59%)
  matrix products  95.9 us (12%)
  local copies, waits for them, and re-layouts  73.3 us (10%)
  waiting for transfers between devices  70.3 us (9%)
  other arithmetic  30.8 us (4%)
  starting transfers between devices  25.3 us (3%)
  between operations  15.5 us (2%)
    dot_general x34, matrix products, apply_full(): jnp.einsum('crs,ncre->ncse', banded, stacked, precision=highest_mode)  80.7 us
    all_gather x3, blocking collectives, body(): lax.all_gather(blocks[1], 'tm', axis=1, tiled=True)  75.7 us
    all_gather x3, blocking collectives, body(): lax.all_gather(blocks[0], 'tm', axis=1, tiled=True)  71.7 us
    all_gather x3, blocking collectives, body(): lax.all_gather(pair[0], 'tm', axis=1, tiled=True)  67.4 us
    reduce_scatter x6, waiting for transfers between devices, carry_prefix(): lax.psum_scatter(term(jnp.int32(0), moved.shape[0] * lax.axis_size('space...  67.1 us
    all_gather x3, blocking collectives, body(): lax.all_gather(pair[1], 'tm', axis=1, tiled=True)  67.1 us
    all_gather x5, blocking collectives, body(): col_trans = lax.all_gather(blocks[0], 'space', axis=0, tiled=True)  66.7 us
    all_gather x5, blocking collectives, body(): col_smooth = lax.all_gather(blocks[1], 'space', axis=0, tiled=True)  49.2 us
  transfers between devices with their start and end apart: 15, of which 6 were waited for; matrix products, arithmetic and copies ran while one was open for 1% of the time, Pallas kernels for 0%

commit v1 on v0

--- a/solution.py
+++ b/solution.py
@@ -3,6 +3,8 @@
 import jax
 import jax.numpy as jnp
 from jax import lax
+from jax.experimental import pallas as pl
+from jax.experimental.pallas import tpu as pltpu
 from jax.sharding import PartitionSpec as P
 
 highest_mode = lax.Precision.HIGHEST
@@ -136,10 +138,358 @@
     smoothed = lax.dynamic_slice_in_dim(smoothed_full, column * tile_width, tile_width, 1)
     return (filtered, smoothed)
 
+MESH = pl.DeviceIdType.MESH
+SUBLANES = 8
+
+
+def pieces(x):
+    high = x.astype(jnp.bfloat16)
+    rest = x - high.astype(jnp.float32)
+    mid = rest.astype(jnp.bfloat16)
+    low = (rest - mid.astype(jnp.float32)).astype(jnp.bfloat16)
+    return high, mid, low
+
+
+def dot(a, b):
+    return jnp.dot(a, b, preferred_element_type=jnp.float32)
+
+
+def times(x, table):
+    rows = x.shape[0]
+    high = x.astype(jnp.bfloat16).astype(jnp.float32)
+    both = jnp.concatenate([high, x - high], 0).astype(jnp.bfloat16)
+    two = dot(both, table[0]) + dot(both, table[1])
+    return two[:rows] + two[rows:] + dot(high.astype(jnp.bfloat16), table[2])
+
+
+def square(table, result):
+    width = table.shape[1]
+    part = min(width, 256)
+
+    def one(index, _):
+        rows = pl.ds(pl.multiple_of(index * part, part), part)
+        high, mid, low = table[0, rows, :], table[1, rows, :], table[2, rows, :]
+        three = dot(jnp.concatenate([high, mid, low], 0), table[0])
+        two = dot(jnp.concatenate([high, mid], 0), table[1])
+        small = three[2 * part :] + two[part:] + dot(high, table[2])
+        total = three[:part] + (two[:part] + three[part : 2 * part] + small)
+        for place, piece in enumerate(pieces(total)):
+            result[place, rows, :] = piece
+        return 0
+
+    lax.fori_loop(0, width // part, one, 0)
+
+
+def swap_halves(x):
+    return pltpu.roll(x, SUBLANES // 2, x.ndim - 2)
+
+
+def upper_half(shape):
+    return lax.broadcasted_iota(jnp.int32, shape, len(shape) - 2) < SUBLANES // 2
+
+
+def interleave(first, second):
+    upper = upper_half(first.shape)
+    return (
+        jnp.where(upper, first, swap_halves(second)),
+        jnp.where(upper, swap_halves(first), second),
+    )
+
+
+def kernel(
+    ranks, columns, observed, gain, trans, dynamics, smooth_gain, filtered, smoothed,
+    outbox, forcing, states, drive, results, inbox_f, inbox_s, entries, summed, raw,
+    trans_1, trans_p, trans_4, trans_8, smooth_1, smooth_4, smooth_8, dyn_1,
+    table_send, table_recv, table_own, force_send, force_recv, filt_send, filt_recv, smoo_send, smoo_recv, own_sem,
+):
+    steps, tile_width, members = observed.shape
+    devices = ranks * columns
+    short = steps // 2
+    state_width = columns * tile_width
+    rank = lax.axis_index("tm")
+    column = lax.axis_index("space")
+    me = rank * columns + column
+    beside = column + 1 - 2 * (column % 2)
+    across = (column + 2) % columns
+
+    barrier = pltpu.get_barrier_semaphore()
+
+    def greet(offset, _):
+        other = (me + offset) % devices
+        pl.semaphore_signal(
+            barrier, inc=1, device_id=(other // columns, other % columns), device_id_type=MESH
+        )
+        return 0
+
+    lax.fori_loop(1, devices, greet, 0)
+
+    sources = (trans, smooth_gain, dynamics)
+    for which, source in enumerate(sources):
+        pltpu.make_async_copy(source.at[0], raw.at[which, column], table_own.at[which]).start()
+
+    groups = members // SUBLANES
+
+    def force(step, _):
+        halves = []
+        for half in range(2):
+            image = observed[half * short + step].T
+            value = jnp.dot(image, gain[0], precision=highest_mode, preferred_element_type=jnp.float32)
+            halves.append(value.reshape(groups, SUBLANES, tile_width))
+        even, odd = interleave(*halves)
+        outbox[:, 0, pl.ds(step, 1)] = even[:, None]
+        outbox[:, 1, pl.ds(step, 1)] = odd[:, None]
+        return 0
+
+    lax.fori_loop(0, short, force, 0)
+    pl.semaphore_wait(barrier, devices - 1)
+
+    def table_copy(which, what, source_column, target):
+        return pltpu.make_async_remote_copy(
+            src_ref=sources[which].at[0] if what < 2 else raw.at[which, source_column],
+            dst_ref=raw.at[which, source_column],
+            send_sem=table_send.at[which, what],
+            recv_sem=table_recv.at[which, what],
+            device_id=(rank, target),
+            device_id_type=MESH,
+        )
+
+    def send_table(which):
+        table_copy(which, 0, column, across).start()
+        table_copy(which, 1, column, beside).start()
+
+    def relay_table(which):
+        table_copy(which, 0, column, across).wait_recv()
+        table_copy(which, 2, across, beside).start()
+
+    def finish_table(which):
+        pltpu.make_async_copy(sources[which].at[0], raw.at[which, column], table_own.at[which]).wait()
+        table_copy(which, 1, column, beside).wait_recv()
+        table_copy(which, 2, across, beside).wait_recv()
+
+    def build(which, table):
+        for tile in range(columns):
+            lanes = slice(tile * tile_width, (tile + 1) * tile_width)
+            for row in range(columns):
+                rows = slice(row * tile_width, (row + 1) * tile_width)
+                shift = row - tile + 1
+                if 0 <= shift <= 2:
+                    block = raw[which, tile, shift * tile_width : (shift + 1) * tile_width, :]
+                    for place, piece in enumerate(pieces(block)):
+                        table[place, rows, lanes] = piece
+                else:
+                    for place in range(3):
+                        table[place, rows, lanes] = jnp.zeros((tile_width, tile_width), jnp.bfloat16)
+
+    def lane_part(index):
+        return pl.ds(pl.multiple_of(index * tile_width, tile_width), tile_width)
+
+    def force_copy(offset):
+        other = (me + offset) % devices
+        return pltpu.make_async_remote_copy(
+            src_ref=outbox.at[other // 2, other % 2],
+            dst_ref=forcing.at[:, rank, :, lane_part(column)],
+            send_sem=force_send.at[offset],
+            recv_sem=force_recv.at[offset],
+            device_id=(other // columns, other % columns),
+            device_id_type=MESH,
+        )
+
+    def result_copy(offset, source, inbox, send, recv):
+        other = (me + offset) % devices
+        return pltpu.make_async_remote_copy(
+            src_ref=source.at[:, other // columns, :, lane_part(other % columns)],
+            dst_ref=inbox.at[me // 2, me % 2],
+            send_sem=send.at[offset],
+            recv_sem=recv.at[offset],
+            device_id=(other // columns, other % columns),
+            device_id_type=MESH,
+        )
+
+    def over_others(act):
+        def one(offset, _):
+            act(offset)
+            return 0
+
+        lax.fori_loop(1, devices, one, 0)
+
+    send_table(0)
+    over_others(lambda offset: force_copy(offset).start())
+    own_force = pltpu.make_async_copy(
+        outbox.at[me // 2, me % 2], forcing.at[:, rank, :, lane_part(column)], own_sem.at[0]
+    )
+    own_force.start()
+    send_table(1)
+    send_table(2)
+
+    relay_table(0)
+    finish_table(0)
+    build(0, trans_1)
+    square(trans_1, trans_p)
+    square(trans_p, trans_4)
+    relay_table(1)
+    relay_table(2)
+    square(trans_4, trans_8)
+    finish_table(1)
+    build(1, smooth_1)
+    square(smooth_1, trans_p)
+    square(trans_p, smooth_4)
+    square(smooth_4, smooth_8)
+    finish_table(2)
+    build(2, dyn_1)
+
+    over_others(lambda offset: force_copy(offset).wait_recv())
+    own_force.wait()
+
+    rows = ranks * SUBLANES
+    whole = (ranks, SUBLANES, state_width)
+
+    def flat(x):
+        return x.reshape(rows, state_width)
+
+    def trial(inputs, order, table):
+        def one(index, current):
+            return times(current, table) + flat(inputs[order(index)])
+
+        return lax.fori_loop(1, short, one, flat(inputs[order(0)]))
+
+    def chain(order, table):
+        entries[order(0)] = jnp.zeros((SUBLANES, state_width), jnp.float32)
+        entries[order(1)] = summed[order(0)]
+
+        def one(index, current):
+            current = times(current, table) + summed[order(index)]
+            entries[order(index + 1)] = current
+            return current
+
+        lax.fori_loop(1, ranks - 1, one, summed[order(0)])
+
+    def final(inputs, order, table, entry, outputs):
+        def one(index, current):
+            current = times(current, table) + flat(inputs[order(index)])
+            outputs[order(index)] = current.reshape(whole)
+            return current
+
+        lax.fori_loop(0, short, one, entry)
+
+    forward = lambda index: index
+    upper = upper_half(whole)
+    ends = trial(forcing, forward, trans_1)
+    halves = ends.reshape(whole)
+    summed[...] = times(ends, trans_4).reshape(whole) + swap_halves(halves)
+    chain(forward, trans_8)
+    first = entries[...]
+    second = times(flat(first), trans_4).reshape(whole) + halves
+    final(forcing, forward, trans_1, flat(jnp.where(upper, first, swap_halves(second))), states)
+
+    over_others(lambda offset: result_copy(offset, states, inbox_f, filt_send, filt_recv).start())
+    own_filtered = pltpu.make_async_copy(
+        states.at[:, rank, :, lane_part(column)], inbox_f.at[me // 2, me % 2], own_sem.at[1]
+    )
+    own_filtered.start()
+
+    def innovate(step, _):
+        value = flat(states[step])
+        mixed = times(times(value, dyn_1), smooth_1)
+        place = lax.broadcasted_iota(jnp.int32, mixed.shape, 0)
+        at_end = jnp.logical_and(place >= rows - SUBLANES // 2, step == short - 1)
+        drive[step] = jnp.where(at_end, value, value - mixed).reshape(whole)
+        return 0
+
+    lax.fori_loop(0, short, innovate, 0)
+
+    backward = lambda index: short - 1 - index
+    heads = trial(drive, backward, smooth_1)
+    halves = heads.reshape(whole)
+    summed[...] = swap_halves(times(heads, smooth_4).reshape(whole)) + halves
+    chain(lambda index: ranks - 1 - index, smooth_8)
+    last = entries[...]
+    before = times(flat(last), smooth_4).reshape(whole) + swap_halves(halves)
+    final(drive, backward, smooth_1, flat(jnp.where(upper, before, swap_halves(last))), results)
+
+    over_others(lambda offset: result_copy(offset, results, inbox_s, smoo_send, smoo_recv).start())
+    own_smoothed = pltpu.make_async_copy(
+        results.at[:, rank, :, lane_part(column)], inbox_s.at[me // 2, me % 2], own_sem.at[2]
+    )
+    own_smoothed.start()
+
+    def deliver(inbox, output):
+        def one(step, _):
+            parts = interleave(inbox[:, 0, step], inbox[:, 1, step])
+            for half, part in enumerate(parts):
+                output[half * short + step] = part.reshape(members, tile_width).T
+            return 0
+
+        lax.fori_loop(0, short, one, 0)
+
+    over_others(lambda offset: result_copy(offset, states, inbox_f, filt_send, filt_recv).wait_recv())
+    own_filtered.wait()
+    deliver(inbox_f, filtered)
+    over_others(lambda offset: result_copy(offset, results, inbox_s, smoo_send, smoo_recv).wait_recv())
+    own_smoothed.wait()
+    deliver(inbox_s, smoothed)
+
+    for which in range(3):
+        table_copy(which, 0, column, across).wait_send()
+        table_copy(which, 1, column, beside).wait_send()
+        table_copy(which, 2, across, beside).wait_send()
+    over_others(lambda offset: force_copy(offset).wait_send())
+    over_others(lambda offset: result_copy(offset, states, inbox_f, filt_send, filt_recv).wait_send())
+    over_others(lambda offset: result_copy(offset, results, inbox_s, smoo_send, smoo_recv).wait_send())
+
+
+def member_body(ranks, columns, observed, gain, trans, dynamics, smooth_gain):
+    steps, tile_width, members = observed.shape
+    devices = ranks * columns
+    short = steps // 2
+    width = columns * tile_width
+    pairs = devices // 2
+    boxes = pltpu.VMEM((pairs, 2, short, SUBLANES, tile_width), jnp.float32)
+    series = pltpu.VMEM((short, ranks, SUBLANES, width), jnp.float32)
+    block = pltpu.VMEM((ranks, SUBLANES, width), jnp.float32)
+    table = pltpu.VMEM((3, width, width), jnp.bfloat16)
+    each = pltpu.SemaphoreType.DMA((devices,))
+    vmem = pl.BlockSpec(memory_space=pltpu.VMEM)
+    return pl.pallas_call(
+        partial(kernel, ranks, columns),
+        out_shape=[jax.ShapeDtypeStruct(observed.shape, jnp.float32)] * 2,
+        in_specs=[vmem] * 5,
+        out_specs=[vmem] * 2,
+        scratch_shapes=[
+            boxes, series, series, series, series, boxes, boxes, block, block,
+            pltpu.VMEM((3, columns, 3 * tile_width, tile_width), jnp.float32),
+            table, table, table, table, table, table, table, table,
+            pltpu.SemaphoreType.DMA((3, 3)),
+            pltpu.SemaphoreType.DMA((3, 3)),
+            pltpu.SemaphoreType.DMA((3,)),
+            each, each, each, each, each, each,
+            pltpu.SemaphoreType.DMA((3,)),
+        ],
+        compiler_params=pltpu.CompilerParams(
+            collective_id=0, has_side_effects=True, vmem_limit_bytes=56 * 2**20
+        ),
+    )(observed, gain, trans, dynamics, smooth_gain)
+
+
+def by_members(mesh, observed, gain, trans, dynamics, smooth_gain):
+    ranks, columns = mesh.shape["tm"], mesh.shape["space"]
+    devices = ranks * columns
+    steps, tile_width, members = observed.shape
+    fits = (
+        members * 2 == devices * SUBLANES
+        and steps % 2 == 0
+        and columns == 4
+        and ranks >= 3
+        and tile_width == 128
+        and members == 128
+    )
+    if fits:
+        return tuple(member_body(ranks, columns, observed, gain, trans, dynamics, smooth_gain))
+    return body(observed, gain, trans, dynamics, smooth_gain)
+
 
 def solution(mesh):
     return jax.shard_map(
-        body,
+        partial(by_members, mesh),
         mesh=mesh,
         in_specs=(
             P("tm", "space", None),

time: 769 us -> 71.3 us (0.09)
  blocking collectives: 450 us -> 0 us
  matrix products: 95.9 us -> 0 us
  local copies, waits for them, and re-layouts: 73.3 us -> 2.73 us
  waiting for transfers between devices: 70.3 us -> 0 us
  Pallas kernels: 0 us -> 67.7 us
  other arithmetic: 30.8 us -> 0 us
  starting transfers between devices: 25.3 us -> 0 us
  between operations: 15.5 us -> 0.65 us
    all_gather x27 -> x0, blocking collectives: 450 us -> none  [the longest x3 75.7 us: body(): lax.all_gather(blocks[1], 'tm', axis=1, tiled=True)]
    dot_general x51 -> x0, matrix products: 95.9 us -> none  [the longest x34 80.7 us: apply_full(): jnp.einsum('crs,ncre->ncse', banded, stacked, precision=highest_mode)]
    pallas_call x0 -> x1, Pallas kernels: none -> 67.7 us  [member_body(): pl.pallas_call(partial(kernel, ranks, columns), out_shape=[jax.ShapeDtype...]
    reduce_scatter x6 -> x0, waiting for transfers between devices: 67.1 us -> none  [carry_prefix(): lax.psum_scatter(term(jnp.int32(0), moved.shape[0] * lax.axis_size('space...]
    another operation x27 -> x0, local copies, waits for them, and re-layouts: 25.8 us -> none  [the longest x16 14.9 us: sweep(): current = apply_step(current[None])[0] + inputs[moment]]
    ppermute x8 -> x0, starting transfers between devices: 25 us -> none  [shifted(): return lax.ppermute(shard, axis, pairs)]
    unnamed x14 -> x0, other arithmetic: 18.3 us -> none
    squeeze x15 -> x0, local copies, waits for them, and re-layouts: 14.8 us -> none  [sweep(): current = apply_step(current[None])[0] + inputs[moment]]
  transfers between devices with their start and end apart: 15 -> 0, of which waited for: 6 -> 0; matrix products, arithmetic and copies ran while one was open for 1% -> 0% of each run, Pallas kernels for 0% -> 0%
where the time goes in v1:
time: 71.3 us; the launch traced here: 71.1 us
  Pallas kernels  67.7 us (95%)
  local copies, waits for them, and re-layouts  2.73 us (4%)
    pallas_call x1, Pallas kernels, member_body(): pl.pallas_call(partial(kernel, ranks, columns), out_shape=[jax.ShapeDtype...  67.7 us
    unnamed x4, local copies, waits for them, and re-layouts  2.73 us

profile of v1, /device:TPU:15, one launch (start us, length us, event | category | flops | bytes accessed | tf_op | source)
XLA Modules:
  0.0 71.1 jit_solution(6826988063413480679)
XLA Ops:
  0.6 67.7 %shard_map.68 = (f32[8,128,128]{2,1,0:T(8,128)}, f32[8,128,128]{2,1,0:T(8,128)}) custom-call(f32[8,128,128]{2,1,0:T(8,128)} %observed.1, f32[1,128,128]{2,1,0:T(8,128)} %gain.1, f32[1,384,128]{2,1,0:T(8,128)} %trans.1, f32[1,384,128]{2,1,0:T(8,128)} %dynamics.1, f32[1,384,128]{2,1,0:T(8,128)} %smooth_gain.1), custom_call_target="tpu_custom_call" | custom-call | tf_op jit(solution)/shard_map/pallas_call | solution.py:452
  68.4 0.0 copy-start
  68.4 1.9 %copy.9 = f32[8,128,128]{2,1,0:T(8,128)} copy(f32[8,128,128]{2,1,0:T(8,128)} %get-tuple-element.4) | data formatting | bytes 1048576
  70.3 0.0 copy-done
  70.3 0.8 %copy.10 = f32[8,128,128]{2,1,0:T(8,128)} copy(f32[8,128,128]{2,1,0:T(8,128)S(1)} %copy-done) | data formatting | bytes 1048576
Async XLA Ops:
  68.4 1.9 %copy-start = (f32[8,128,128]{2,1,0:T(8,128)S(1)}, f32[8,128,128]{2,1,0:T(8,128)}, u32[]{:S(2)}) copy-start(f32[8,128,128]{2,1,0:T(8,128)} %get-tuple-element.5) | copy-start | bytes 1572868

commit v2 on v1

--- a/solution.py
+++ b/solution.py
@@ -140,14 +140,12 @@
 
 MESH = pl.DeviceIdType.MESH
 SUBLANES = 8
+SPLIT = (1, 2)
 
 
 def pieces(x):
     high = x.astype(jnp.bfloat16)
-    rest = x - high.astype(jnp.float32)
-    mid = rest.astype(jnp.bfloat16)
-    low = (rest - mid.astype(jnp.float32)).astype(jnp.bfloat16)
-    return high, mid, low
+    return high, (x - high.astype(jnp.float32)).astype(jnp.bfloat16)
 
 
 def dot(a, b):
@@ -159,7 +157,7 @@
     high = x.astype(jnp.bfloat16).astype(jnp.float32)
     both = jnp.concatenate([high, x - high], 0).astype(jnp.bfloat16)
     two = dot(both, table[0]) + dot(both, table[1])
-    return two[:rows] + two[rows:] + dot(high.astype(jnp.bfloat16), table[2])
+    return two[:rows] + two[rows:]
 
 
 def square(table, result):
@@ -168,11 +166,9 @@
 
     def one(index, _):
         rows = pl.ds(pl.multiple_of(index * part, part), part)
-        high, mid, low = table[0, rows, :], table[1, rows, :], table[2, rows, :]
-        three = dot(jnp.concatenate([high, mid, low], 0), table[0])
-        two = dot(jnp.concatenate([high, mid], 0), table[1])
-        small = three[2 * part :] + two[part:] + dot(high, table[2])
-        total = three[:part] + (two[:part] + three[part : 2 * part] + small)
+        high, low = table[0, rows, :], table[1, rows, :]
+        two = dot(jnp.concatenate([high, low], 0), table[0])
+        total = two[:part] + (two[part:] + dot(high, table[1]))
         for place, piece in enumerate(pieces(total)):
             result[place, rows, :] = piece
         return 0
@@ -243,28 +239,58 @@
     lax.fori_loop(0, short, force, 0)
     pl.semaphore_wait(barrier, devices - 1)
 
-    def table_copy(which, what, source_column, target):
+    shared = rank % 2
+    partner = rank + 1 - 2 * shared
+
+    def half_rows(index):
+        count = 3 * tile_width // 2
+        return pl.ds(pl.multiple_of(index * count, count), count)
+
+    def table_copy(which, what):
+        split = which in SPLIT
+        if what == 0:
+            place, to = column, (rank, across)
+            rows = half_rows(shared) if split else slice(None)
+        elif what == 1:
+            place, to, rows = column, (rank, beside), slice(None)
+        elif what == 2:
+            place, to = across, (rank, beside)
+            rows = half_rows(shared) if split else slice(None)
+        elif what == 3:
+            place, to, rows = across, (partner, column), half_rows(shared)
+        else:
+            place, to, rows = across, (rank, beside), half_rows(1 - shared)
+        source = sources[which].at[0, rows] if what < 2 else raw.at[which, place, rows]
         return pltpu.make_async_remote_copy(
-            src_ref=sources[which].at[0] if what < 2 else raw.at[which, source_column],
-            dst_ref=raw.at[which, source_column],
+            src_ref=source,
+            dst_ref=raw.at[which, place, rows],
             send_sem=table_send.at[which, what],
             recv_sem=table_recv.at[which, what],
-            device_id=(rank, target),
+            device_id=to,
             device_id_type=MESH,
         )
 
     def send_table(which):
-        table_copy(which, 0, column, across).start()
-        table_copy(which, 1, column, beside).start()
+        table_copy(which, 0).start()
+        table_copy(which, 1).start()
 
     def relay_table(which):
-        table_copy(which, 0, column, across).wait_recv()
-        table_copy(which, 2, across, beside).start()
+        table_copy(which, 0).wait_recv()
+        table_copy(which, 2).start()
+        if which in SPLIT:
+            table_copy(which, 3).start()
+
+    def relay_again(which):
+        if which in SPLIT:
+            table_copy(which, 3).wait_recv()
+            table_copy(which, 4).start()
 
     def finish_table(which):
         pltpu.make_async_copy(sources[which].at[0], raw.at[which, column], table_own.at[which]).wait()
-        table_copy(which, 1, column, beside).wait_recv()
-        table_copy(which, 2, across, beside).wait_recv()
+        table_copy(which, 1).wait_recv()
+        table_copy(which, 2).wait_recv()
+        if which in SPLIT:
+            table_copy(which, 4).wait_recv()
 
     def build(which, table):
         for tile in range(columns):
@@ -277,7 +303,7 @@
                     for place, piece in enumerate(pieces(block)):
                         table[place, rows, lanes] = piece
                 else:
-                    for place in range(3):
+                    for place in range(2):
                         table[place, rows, lanes] = jnp.zeros((tile_width, tile_width), jnp.bfloat16)
 
     def lane_part(index):
@@ -326,9 +352,61 @@
     build(0, trans_1)
     square(trans_1, trans_p)
     square(trans_p, trans_4)
+    square(trans_4, trans_8)
+    over_others(lambda offset: force_copy(offset).wait_recv())
+    own_force.wait()
+
     relay_table(1)
+    rows = ranks * SUBLANES
+    whole = (ranks, SUBLANES, state_width)
+
+    def flat(x):
+        return x.reshape(rows, state_width)
+
+    def trial(inputs, order, table):
+        def one(index, current):
+            return times(current, table) + flat(inputs[order(index)])
+
+        return lax.fori_loop(1, short, one, flat(inputs[order(0)]))
+
+    def chain(order, table):
+        entries[order(0)] = jnp.zeros((SUBLANES, state_width), jnp.float32)
+        entries[order(1)] = summed[order(0)]
+
+        def one(index, current):
+            current = times(current, table) + summed[order(index)]
+            entries[order(index + 1)] = current
+            return current
+
+        lax.fori_loop(1, ranks - 1, one, summed[order(0)])
+
+    def final(inputs, order, table, entry, outputs):
+        def one(index, current):
+            current = times(current, table) + flat(inputs[order(index)])
+            outputs[order(index)] = current.reshape(whole)
+            return current
+
+        lax.fori_loop(0, short, one, entry)
+
+    forward = lambda index: index
+    upper = upper_half(whole)
+    ends = trial(forcing, forward, trans_1)
+    halves = ends.reshape(whole)
+    summed[...] = times(ends, trans_4).reshape(whole) + swap_halves(halves)
     relay_table(2)
-    square(trans_4, trans_8)
+    relay_again(1)
+    chain(forward, trans_8)
+    first = entries[...]
+    second = times(flat(first), trans_4).reshape(whole) + halves
+    relay_again(2)
+    final(forcing, forward, trans_1, flat(jnp.where(upper, first, swap_halves(second))), states)
+
+    over_others(lambda offset: result_copy(offset, states, inbox_f, filt_send, filt_recv).start())
+    own_filtered = pltpu.make_async_copy(
+        states.at[:, rank, :, lane_part(column)], inbox_f.at[me // 2, me % 2], own_sem.at[1]
+    )
+    own_filtered.start()
+
     finish_table(1)
     build(1, smooth_1)
     square(smooth_1, trans_p)
@@ -336,56 +414,6 @@
     square(smooth_4, smooth_8)
     finish_table(2)
     build(2, dyn_1)
-
-    over_others(lambda offset: force_copy(offset).wait_recv())
-    own_force.wait()
-
-    rows = ranks * SUBLANES
-    whole = (ranks, SUBLANES, state_width)
-
-    def flat(x):
-        return x.reshape(rows, state_width)
-
-    def trial(inputs, order, table):
-        def one(index, current):
-            return times(current, table) + flat(inputs[order(index)])
-
-        return lax.fori_loop(1, short, one, flat(inputs[order(0)]))
-
-    def chain(order, table):
-        entries[order(0)] = jnp.zeros((SUBLANES, state_width), jnp.float32)
-        entries[order(1)] = summed[order(0)]
-
-        def one(index, current):
-            current = times(current, table) + summed[order(index)]
-            entries[order(index + 1)] = current
-            return current
-
-        lax.fori_loop(1, ranks - 1, one, summed[order(0)])
-
-    def final(inputs, order, table, entry, outputs):
-        def one(index, current):
-            current = times(current, table) + flat(inputs[order(index)])
-            outputs[order(index)] = current.reshape(whole)
-            return current
-
-        lax.fori_loop(0, short, one, entry)
-
-    forward = lambda index: index
-    upper = upper_half(whole)
-    ends = trial(forcing, forward, trans_1)
-    halves = ends.reshape(whole)
-    summed[...] = times(ends, trans_4).reshape(whole) + swap_halves(halves)
-    chain(forward, trans_8)
-    first = entries[...]
-    second = times(flat(first), trans_4).reshape(whole) + halves
-    final(forcing, forward, trans_1, flat(jnp.where(upper, first, swap_halves(second))), states)
-
-    over_others(lambda offset: result_copy(offset, states, inbox_f, filt_send, filt_recv).start())
-    own_filtered = pltpu.make_async_copy(
-        states.at[:, rank, :, lane_part(column)], inbox_f.at[me // 2, me % 2], own_sem.at[1]
-    )
-    own_filtered.start()
 
     def innovate(step, _):
         value = flat(states[step])
@@ -429,9 +457,8 @@
     deliver(inbox_s, smoothed)
 
     for which in range(3):
-        table_copy(which, 0, column, across).wait_send()
-        table_copy(which, 1, column, beside).wait_send()
-        table_copy(which, 2, across, beside).wait_send()
+        for what in range(5 if which in SPLIT else 3):
+            table_copy(which, what).wait_send()
     over_others(lambda offset: force_copy(offset).wait_send())
     over_others(lambda offset: result_copy(offset, states, inbox_f, filt_send, filt_recv).wait_send())
     over_others(lambda offset: result_copy(offset, results, inbox_s, smoo_send, smoo_recv).wait_send())
@@ -446,7 +473,7 @@
     boxes = pltpu.VMEM((pairs, 2, short, SUBLANES, tile_width), jnp.float32)
     series = pltpu.VMEM((short, ranks, SUBLANES, width), jnp.float32)
     block = pltpu.VMEM((ranks, SUBLANES, width), jnp.float32)
-    table = pltpu.VMEM((3, width, width), jnp.bfloat16)
+    table = pltpu.VMEM((2, width, width), jnp.bfloat16)
     each = pltpu.SemaphoreType.DMA((devices,))
     vmem = pl.BlockSpec(memory_space=pltpu.VMEM)
     return pl.pallas_call(
@@ -458,8 +485,8 @@
             boxes, series, series, series, series, boxes, boxes, block, block,
             pltpu.VMEM((3, columns, 3 * tile_width, tile_width), jnp.float32),
             table, table, table, table, table, table, table, table,
-            pltpu.SemaphoreType.DMA((3, 3)),
-            pltpu.SemaphoreType.DMA((3, 3)),
+            pltpu.SemaphoreType.DMA((3, 5)),
+            pltpu.SemaphoreType.DMA((3, 5)),
             pltpu.SemaphoreType.DMA((3,)),
             each, each, each, each, each, each,
             pltpu.SemaphoreType.DMA((3,)),

time: 71.3 us -> 59.7 us (0.84)
  Pallas kernels: 67.7 us -> 56.1 us
    pallas_call x1, Pallas kernels: 67.7 us -> 56.1 us  [member_body(): pl.pallas_call(partial(kernel, ranks, columns), out_shape=[jax.ShapeDtype...]
where the time goes in v2:
time: 59.7 us; the launch traced here: 59.5 us
  Pallas kernels  56.1 us (94%)
  local copies, waits for them, and re-layouts  2.73 us (5%)
  between operations  0.65 us (1%)
    pallas_call x1, Pallas kernels, member_body(): pl.pallas_call(partial(kernel, ranks, columns), out_shape=[jax.ShapeDtype...  56.1 us
    unnamed x4, local copies, waits for them, and re-layouts  2.73 us

profile of v2, /device:TPU:15, one launch (start us, length us, event | category | flops | bytes accessed | tf_op | source)
XLA Modules:
  0.0 59.5 jit_solution(11277564603854149570)
XLA Ops:
  0.6 56.1 %shard_map.68 = (f32[8,128,128]{2,1,0:T(8,128)}, f32[8,128,128]{2,1,0:T(8,128)}) custom-call(f32[8,128,128]{2,1,0:T(8,128)} %observed.1, f32[1,128,128]{2,1,0:T(8,128)} %gain.1, f32[1,384,128]{2,1,0:T(8,128)} %trans.1, f32[1,384,128]{2,1,0:T(8,128)} %dynamics.1, f32[1,384,128]{2,1,0:T(8,128)} %smooth_gain.1), custom_call_target="tpu_custom_call" | custom-call | tf_op jit(solution)/shard_map/pallas_call | solution.py:479
  56.8 0.0 copy-start
  56.8 1.9 %copy.9 = f32[8,128,128]{2,1,0:T(8,128)} copy(f32[8,128,128]{2,1,0:T(8,128)} %get-tuple-element.4) | data formatting | bytes 1048576
  58.7 0.0 copy-done
  58.7 0.8 %copy.10 = f32[8,128,128]{2,1,0:T(8,128)} copy(f32[8,128,128]{2,1,0:T(8,128)S(1)} %copy-done) | data formatting | bytes 1048576
Async XLA Ops:
  56.8 1.9 %copy-start = (f32[8,128,128]{2,1,0:T(8,128)S(1)}, f32[8,128,128]{2,1,0:T(8,128)}, u32[]{:S(2)}) copy-start(f32[8,128,128]{2,1,0:T(8,128)} %get-tuple-element.5) | copy-start | bytes 1572868

commit v3 on v2

--- a/solution.py
+++ b/solution.py
@@ -225,11 +225,14 @@
 
     groups = members // SUBLANES
 
+    gain_high, gain_low = pieces(gain[0])
+
     def force(step, _):
         halves = []
         for half in range(2):
             image = observed[half * short + step].T
-            value = jnp.dot(image, gain[0], precision=highest_mode, preferred_element_type=jnp.float32)
+            high, low = pieces(image)
+            value = dot(high, gain_high) + (dot(low, gain_high) + dot(high, gain_low))
             halves.append(value.reshape(groups, SUBLANES, tile_width))
         even, odd = interleave(*halves)
         outbox[:, 0, pl.ds(step, 1)] = even[:, None]

time: 59.7 us -> 59.6 us (level)
  no operation moved by 1% of the time
where the time goes in v3:
time: 59.6 us; the launch traced here: 59.5 us
  Pallas kernels  56.1 us (94%)
  local copies, waits for them, and re-layouts  2.73 us (5%)
  between operations  0.65 us (1%)
    pallas_call x1, Pallas kernels, member_body(): pl.pallas_call(partial(kernel, ranks, columns), out_shape=[jax.ShapeDtype...  56.1 us
    unnamed x4, local copies, waits for them, and re-layouts  2.73 us

profile of v3, /device:TPU:15, one launch (start us, length us, event | category | flops | bytes accessed | tf_op | source)
XLA Modules:
  0.0 59.5 jit_solution(8762282189873110575)
XLA Ops:
  0.6 56.1 %shard_map.68 = (f32[8,128,128]{2,1,0:T(8,128)}, f32[8,128,128]{2,1,0:T(8,128)}) custom-call(f32[8,128,128]{2,1,0:T(8,128)} %observed.1, f32[1,128,128]{2,1,0:T(8,128)} %gain.1, f32[1,384,128]{2,1,0:T(8,128)} %trans.1, f32[1,384,128]{2,1,0:T(8,128)} %dynamics.1, f32[1,384,128]{2,1,0:T(8,128)} %smooth_gain.1), custom_call_target="tpu_custom_call" | custom-call | tf_op jit(solution)/shard_map/pallas_call | solution.py:482
  56.7 0.0 copy-start
  56.7 1.9 %copy.9 = f32[8,128,128]{2,1,0:T(8,128)} copy(f32[8,128,128]{2,1,0:T(8,128)} %get-tuple-element.4) | data formatting | bytes 1048576
  58.7 0.0 copy-done
  58.7 0.8 %copy.10 = f32[8,128,128]{2,1,0:T(8,128)} copy(f32[8,128,128]{2,1,0:T(8,128)S(1)} %copy-done) | data formatting | bytes 1048576
Async XLA Ops:
  56.7 1.9 %copy-start = (f32[8,128,128]{2,1,0:T(8,128)S(1)}, f32[8,128,128]{2,1,0:T(8,128)}, u32[]{:S(2)}) copy-start(f32[8,128,128]{2,1,0:T(8,128)} %get-tuple-element.5) | copy-start | bytes 1572868
